TPU v7x, 32 devices: a whole 2x2x4 slice. The times are simulated.
32 devices in a mesh: row: 4 (over y, core), col: 8 (over z, x).
Axes of the slice: x: 2, y: 2, z: 4, core: 2. Of those that a mesh axis runs over, the one named last changes fastest.
Arguments:
- blocks: float32 [4096, 128, 128], P(('row', 'col')), may hold values from -0.25 to 0.25
- block_rows: int32 [32, 128], P(('row', 'col')), may hold values from 0 to 1023, as said below
- block_cols: int32 [32, 128], P(('row', 'col')), may hold values from 0 to 511
- diagonal: float32 [524288], P(('row', 'col')), may hold values from 1 to 4
- right_sides: float32 [2, 524288], P(None, ('row', 'col')), may hold values from -6 to 6
Outputs:
- solution: float32 [2, 524288], P(None, ('row', 'col'))
- hessenberg: float32 [2, 9, 8], replicated
Inputs may be any that keep to these rules, and one draw needn't show every extreme that they name: `block_rows`: non-decreasing along each tile's slots; a local block row may hold no stored block.
All inputs are finite; a program needn't handle non-finite values.
Results may differ from a plain program's by a relative error of at most 0.0085.
Values sent between devices are 32-bit elements; how exact they have to be, the bound alone decides.
A program may use at most 128 MiB of HBM per device.

v0:
```python
import jax
import jax.numpy as jnp
from jax import lax
from jax.sharding import PartitionSpec as P

STEPS = 8
epsilon = 1e-06


def least_squares(hessenberg, initial_norm):
    total_steps = hessenberg.shape[2]
    targets = [initial_norm] + [jnp.zeros_like(initial_norm) for j in range(total_steps)]
    cosines, sines, triangle = ([], [], [])
    for j in range(total_steps):
        column = [hessenberg[:, i, j] for i in range(j + 2)]
        for i in range(j):
            leading, trailing = (column[i], column[i + 1])
            column[i] = cosines[i] * leading + sines[i] * trailing
            column[i + 1] = cosines[i] * trailing - sines[i] * leading
        radius = jnp.sqrt(column[j] * column[j] + column[j + 1] * column[j + 1])
        cosine = column[j] / radius
        sine_term = column[j + 1] / radius
        column[j] = radius
        cosines.append(cosine)
        sines.append(sine_term)
        targets[j + 1] = -sine_term * targets[j]
        targets[j] = cosine * targets[j]
        triangle.append(column[: j + 1])
    coeffs = [None] * total_steps
    for j in reversed(range(total_steps)):
        running = targets[j]
        for k in range(j + 1, total_steps):
            running = running - triangle[k][j] * coeffs[k]
        coeffs[j] = running / triangle[j][j]
    return jnp.stack(coeffs, axis=1)


def apply_matrix(vector, blocks, rows_onehot, block_cols, diagonal):
    systems = vector.shape[0]
    width = blocks.shape[1]
    gathered = lax.all_gather(vector, "row", axis=1, tiled=True)
    grouped = gathered.reshape(systems, -1, width)
    picked = jnp.take(grouped, block_cols, axis=1)
    products = jnp.einsum("kij,nkj->nki", blocks, picked, precision=lax.Precision.HIGHEST)
    own_rows = lax.psum_scatter(
        jnp.einsum("mk,nki->mni", rows_onehot, products, precision=lax.Precision.HIGHEST),
        "col",
        scatter_dimension=0,
        tiled=True,
    )
    summed = jnp.transpose(own_rows, (1, 0, 2)).reshape(systems, -1)
    return diagonal[None, :] * vector + summed


def body(blocks, block_rows, block_cols, diagonal, right_sides):
    systems = right_sides.shape[0]
    width = blocks.shape[1]
    row_count = lax.axis_size("col") * (right_sides.shape[1] // width)
    positions = jnp.arange(row_count, dtype=jnp.int32)
    rows_onehot = (block_rows[0][None, :] == positions[:, None]).astype(jnp.float32)
    columns_local = block_cols[0]
    total_steps = STEPS
    initial_norm = jnp.sqrt(
        lax.psum(jnp.sum(right_sides * right_sides, axis=1), ("row", "col")) + epsilon
    )
    krylov_basis = [right_sides / initial_norm[:, None]]
    hessenberg = jnp.zeros((systems, total_steps + 1, total_steps), jnp.float32)
    for j in range(total_steps):
        candidate = apply_matrix(krylov_basis[j], blocks, rows_onehot, columns_local, diagonal)
        stacked = jnp.stack(krylov_basis)
        local_dots = jnp.einsum("inl,nl->ni", stacked, candidate, precision=lax.Precision.HIGHEST)
        coeffs = lax.psum(local_dots, ("row", "col"))
        candidate = candidate - jnp.einsum(
            "ni,inl->nl", coeffs, stacked, precision=lax.Precision.HIGHEST
        )
        remainder_sq = lax.psum(jnp.sum(candidate * candidate, axis=1), ("row", "col"))
        new_norm = jnp.sqrt(remainder_sq + epsilon)
        hessenberg = hessenberg.at[:, : j + 1, j].set(coeffs)
        hessenberg = hessenberg.at[:, j + 1, j].set(new_norm)
        krylov_basis.append(candidate / new_norm[:, None])
    weights = least_squares(hessenberg, initial_norm)
    solution = jnp.einsum(
        "ni,inl->nl",
        weights,
        jnp.stack(krylov_basis[:total_steps]),
        precision=lax.Precision.HIGHEST,
    )
    return (solution, hessenberg)


def solution(mesh):
    return jax.shard_map(
        body,
        mesh=mesh,
        in_specs=(
            P(("row", "col"), None, None),
            P(("row", "col"), None),
            P(("row", "col"), None),
            P(("row", "col")),
            P(None, ("row", "col")),
        ),
        out_specs=(P(None, ("row", "col")), P()),
        check_vma=False,
    )
```

profile of v0, /device:TPU:0, one launch (start us, length us, event | category | flops | bytes accessed | tf_op | source)
XLA Modules:
  0.0 1472.0 jit_solution(12052770710032486379)
XLA Ops:
  9.7 41.9 %psum.119 = f32[2]{0:T(128)S(1)} all-reduce(f32[2]{0:T(128)S(1)} %multiply_reduce_fusion.8), channel_id=1, replica_groups=mesh['row'=4,'col'=8] {'row','col'}, use_global_device_ids=true, to_apply=%region_1.0 | all-reduce | flops 2 | bytes 16 | tf_op jit(solution)/shard_map/psum | solution.py:64
  79.3 62.7 %reduce-scatter.9.cloned.1.call-done = f32[128,2,128]{2,0,1:T(8,128)} async-done(((f32[1024,2,128]{2,0,1:T(8,128)}), f32[128,2,128]{2,0,1:T(8,128)}) %reduce-scatter.9.cloned.1.call-update) | async-done | bytes 131088 | tf_op jit(solution)/shard_map/reduce_scatter | solution.py:45
  143.1 39.9 %psum.120 = f32[2,1]{0,1:T(1,128)S(1)} all-reduce(f32[2,1]{0,1:T(1,128)S(1)} %bitcast.742), channel_id=1, replica_groups=mesh['row'=4,'col'=8] {'row','col'}, use_global_device_ids=true, to_apply=%region_3.5 | all-reduce | flops 2 | bytes 16 | tf_op jit(solution)/shard_map/psum | solution.py:72
  184.2 39.2 %psum.121 = f32[2]{0:T(128)S(1)} all-reduce(f32[2]{0:T(128)S(1)} %get-tuple-element.266), channel_id=1, replica_groups=mesh['row'=4,'col'=8] {'row','col'}, use_global_device_ids=true, to_apply=%region_5.7 | all-reduce | flops 2 | bytes 16 | tf_op jit(solution)/shard_map/psum | solution.py:76
  251.0 61.7 %reduce-scatter.11.cloned.1.call-done = f32[128,2,128]{2,0,1:T(8,128)} async-done(((f32[1024,2,128]{2,0,1:T(8,128)}), f32[128,2,128]{2,0,1:T(8,128)}) %reduce-scatter.11.cloned.1.call-update) | async-done | bytes 131088 | tf_op jit(solution)/shard_map/reduce_scatter | solution.py:45
  316.2 39.8 %psum.122 = f32[2,2]{1,0:T(2,128)S(1)} all-reduce(f32[2,2]{1,0:T(2,128)S(1)} %bitcast.732), channel_id=1, replica_groups=mesh['row'=4,'col'=8] {'row','col'}, use_global_device_ids=true, to_apply=%region_7.9 | all-reduce | flops 4 | bytes 32 | tf_op jit(solution)/shard_map/psum | solution.py:72
  357.4 39.2 %psum.123 = f32[2]{0:T(128)S(1)} all-reduce(f32[2]{0:T(128)S(1)} %multiply_reduce_fusion.6), channel_id=1, replica_groups=mesh['row'=4,'col'=8] {'row','col'}, use_global_device_ids=true, to_apply=%region_9.11 | all-reduce | flops 2 | bytes 16 | tf_op jit(solution)/shard_map/psum | solution.py:76
  425.1 61.8 %reduce-scatter.13.cloned.1.call-done = f32[128,2,128]{2,0,1:T(8,128)} async-done(((f32[1024,2,128]{2,0,1:T(8,128)}), f32[128,2,128]{2,0,1:T(8,128)}) %reduce-scatter.13.cloned.1.call-update) | async-done | bytes 131088 | tf_op jit(solution)/shard_map/reduce_scatter | solution.py:45
  490.4 39.8 %psum.124 = f32[2,3]{1,0:T(2,128)S(1)} all-reduce(f32[2,3]{1,0:T(2,128)S(1)} %bitcast.733), channel_id=1, replica_groups=mesh['row'=4,'col'=8] {'row','col'}, use_global_device_ids=true, to_apply=%region_12.14 | all-reduce | flops 6 | bytes 48 | tf_op jit(solution)/shard_map/psum | solution.py:72
  532.7 39.2 %psum.125 = f32[2]{0:T(128)S(1)} all-reduce(f32[2]{0:T(128)S(1)} %multiply_reduce_fusion.5), channel_id=1, replica_groups=mesh['row'=4,'col'=8] {'row','col'}, use_global_device_ids=true, to_apply=%region_14.16 | all-reduce | flops 2 | bytes 16 | tf_op jit(solution)/shard_map/psum | solution.py:76
  602.6 61.4 %reduce-scatter.15.cloned.1.call-done = f32[128,2,128]{2,0,1:T(8,128)} async-done(((f32[1024,2,128]{2,0,1:T(8,128)}), f32[128,2,128]{2,0,1:T(8,128)}) %reduce-scatter.15.cloned.1.call-update) | async-done | bytes 131088 | tf_op jit(solution)/shard_map/reduce_scatter | solution.py:45
  668.6 39.8 %psum.126 = f32[2,4]{1,0:T(2,128)S(1)} all-reduce(f32[2,4]{1,0:T(2,128)S(1)} %bitcast.734), channel_id=1, replica_groups=mesh['row'=4,'col'=8] {'row','col'}, use_global_device_ids=true, to_apply=%region_17.19 | all-reduce | flops 8 | bytes 64 | tf_op jit(solution)/shard_map/psum | solution.py:72
  782.3 62.2 %reduce-scatter.17.cloned.1.call-done = f32[128,2,128]{2,0,1:T(8,128)} async-done(((f32[1024,2,128]{2,0,1:T(8,128)}), f32[128,2,128]{2,0,1:T(8,128)}) %reduce-scatter.17.cloned.1.call-update) | async-done | bytes 131088 | tf_op jit(solution)/shard_map/reduce_scatter | solution.py:45
  848.9 39.8 %psum.128 = f32[2,5]{1,0:T(2,128)S(1)} all-reduce(f32[2,5]{1,0:T(2,128)S(1)} %bitcast.727), channel_id=1, replica_groups=mesh['row'=4,'col'=8] {'row','col'}, use_global_device_ids=true, to_apply=%region_22.24 | all-reduce | flops 10 | bytes 80 | tf_op jit(solution)/shard_map/psum | solution.py:72
  891.8 39.3 %psum.129 = f32[2]{0:T(128)S(1)} all-reduce(f32[2]{0:T(128)S(1)} %multiply_reduce_fusion.3), channel_id=1, replica_groups=mesh['row'=4,'col'=8] {'row','col'}, use_global_device_ids=true, to_apply=%region_24.26 | all-reduce | flops 2 | bytes 16 | tf_op jit(solution)/shard_map/psum | solution.py:76
  959.1 63.2 %reduce-scatter.19.cloned.1.call-done = f32[128,2,128]{2,0,1:T(8,128)} async-done(((f32[1024,2,128]{2,0,1:T(8,128)}), f32[128,2,128]{2,0,1:T(8,128)}) %reduce-scatter.19.cloned.1.call-update) | async-done | bytes 131088 | tf_op jit(solution)/shard_map/reduce_scatter | solution.py:45
  1026.2 39.8 %psum.130 = f32[2,6]{1,0:T(2,128)S(1)} all-reduce(f32[2,6]{1,0:T(2,128)S(1)} %bitcast.728), channel_id=1, replica_groups=mesh['row'=4,'col'=8] {'row','col'}, use_global_device_ids=true, to_apply=%region_27.29 | all-reduce | flops 12 | bytes 96 | tf_op jit(solution)/shard_map/psum | solution.py:72
  1068.3 39.2 %psum.131 = f32[2]{0:T(128)S(1)} all-reduce(f32[2]{0:T(128)S(1)} %multiply_reduce_fusion.2), channel_id=1, replica_groups=mesh['row'=4,'col'=8] {'row','col'}, use_global_device_ids=true, to_apply=%region_29.31 | all-reduce | flops 2 | bytes 16 | tf_op jit(solution)/shard_map/psum | solution.py:76
  1134.0 63.2 %reduce-scatter.21.cloned.1.call-done = f32[128,2,128]{2,0,1:T(8,128)} async-done(((f32[1024,2,128]{2,0,1:T(8,128)}), f32[128,2,128]{2,0,1:T(8,128)}) %reduce-scatter.21.cloned.1.call-update) | async-done | bytes 131088 | tf_op jit(solution)/shard_map/reduce_scatter | solution.py:45
  1201.2 39.9 %psum.132 = f32[2,7]{1,0:T(2,128)S(1)} all-reduce(f32[2,7]{1,0:T(2,128)S(1)} %bitcast.729), channel_id=1, replica_groups=mesh['row'=4,'col'=8] {'row','col'}, use_global_device_ids=true, to_apply=%region_32.34 | all-reduce | flops 14 | bytes 112 | tf_op jit(solution)/shard_map/psum | solution.py:72
  1242.8 39.2 %psum.133 = f32[2]{0:T(128)S(1)} all-reduce(f32[2]{0:T(128)S(1)} %multiply_reduce_fusion.1), channel_id=1, replica_groups=mesh['row'=4,'col'=8] {'row','col'}, use_global_device_ids=true, to_apply=%region_34.36 | all-reduce | flops 2 | bytes 16 | tf_op jit(solution)/shard_map/psum | solution.py:76
  1332.2 39.3 %reduce-scatter.23.cloned.1.call-done = f32[128,2,128]{2,0,1:T(8,128)} async-done(((f32[1024,2,128]{2,0,1:T(8,128)}), f32[128,2,128]{2,0,1:T(8,128)}) %reduce-scatter.23.cloned.1.call-update) | async-done | bytes 131088 | tf_op jit(solution)/shard_map/reduce_scatter | solution.py:45
  1375.6 39.8 %psum.134 = f32[2,8]{1,0:T(2,128)S(1)} all-reduce(f32[2,8]{1,0:T(2,128)S(1)} %bitcast.726), channel_id=1, replica_groups=mesh['row'=4,'col'=8] {'row','col'}, use_global_device_ids=true, to_apply=%region_37.39 | all-reduce | flops 16 | bytes 128 | tf_op jit(solution)/shard_map/psum | solution.py:72
  1418.4 39.2 %psum.135 = f32[2]{0:T(128)S(1)} all-reduce(f32[2]{0:T(128)S(1)} %fusion.56), channel_id=1, replica_groups=mesh['row'=4,'col'=8] {'row','col'}, use_global_device_ids=true, to_apply=%region_39.41 | all-reduce | flops 2 | bytes 16 | tf_op jit(solution)/shard_map/psum | solution.py:76
  (205 shorter events, 346.6 us)
Async XLA Ops:
  7.2 69.7 %copy-start.8 = (s32[1,128]{1,0:T(1,128)S(1)}, s32[1,128]{1,0:T(1,128)}, u32[]{:S(2)}) copy-start(s32[1,128]{1,0:T(1,128)} %param.40) | copy-start | bytes 1540
  7.2 134.8 %copy-start = (f32[16384]{0:T(1024)S(1)}, f32[16384]{0:T(1024)}, u32[]{:S(2)}) copy-start(f32[16384]{0:T(1024)} %param.42) | copy-start | bytes 196612
  7.2 134.8 %reduce-scatter.9.cloned.1.call-start = ((), (), s32[]{:S(2)}) async-start(), calls=%async_computation.8 | async-start | bytes 1179648 | tf_op jit(solution)/shard_map/reduce_scatter | solution.py:45
  78.5 234.2 %reduce-scatter.11.cloned.1.call-start = ((), (), s32[]{:S(2)}) async-start(), calls=%async_computation.9 | async-start | bytes 1179648 | tf_op jit(solution)/shard_map/reduce_scatter | solution.py:45
  249.6 237.3 %reduce-scatter.13.cloned.1.call-start = ((), (), s32[]{:S(2)}) async-start(), calls=%async_computation.10 | async-start | bytes 1179648 | tf_op jit(solution)/shard_map/reduce_scatter | solution.py:45
  423.5 240.4 %reduce-scatter.15.cloned.1.call-start = ((), (), s32[]{:S(2)}) async-start(), calls=%async_computation.11 | async-start | bytes 1179648 | tf_op jit(solution)/shard_map/reduce_scatter | solution.py:45
  531.3 0.7 copy-start.6
  600.7 243.8 %reduce-scatter.17.cloned.1.call-start = ((), (), s32[]{:S(2)}) async-start(), calls=%async_computation.12 | async-start | bytes 1179648 | tf_op jit(solution)/shard_map/reduce_scatter | solution.py:45
  665.0 46.0 %copy-start.4 = (f32[2,16384]{1,0:T(2,128)}, f32[2,16384]{1,0:T(2,128)S(1)}, u32[]{:S(2)}) copy-start(f32[2,16384]{1,0:T(2,128)S(1)} %bitcast_add_fusion.4) | copy-start | bytes 393220
  710.8 0.6 copy-start.5
  712.2 69.1 %copy-start.1 = (f32[7,2,16384]{2,1,0:T(2,128)S(1)}, f32[7,2,16384]{2,1,0:T(2,128)}, u32[]{:S(2)}) copy-start(f32[7,2,16384]{2,1,0:T(2,128)} %get-tuple-element.273) | copy-start | bytes 2752516
  752.5 0.7 copy-start.2
  781.2 241.0 %reduce-scatter.19.cloned.1.call-start = ((), (), s32[]{:S(2)}) async-start(), calls=%async_computation.13 | async-start | bytes 1179648 | tf_op jit(solution)/shard_map/reduce_scatter | solution.py:45
  845.6 0.7 copy-start.3
  890.0 0.6 copy-start.7
  958.9 238.3 %reduce-scatter.21.cloned.1.call-start = ((), (), s32[]{:S(2)}) async-start(), calls=%async_computation.14 | async-start | bytes 1179648 | tf_op jit(solution)/shard_map/reduce_scatter | solution.py:45
  1133.8 175.5 %copy-start.14 = (s32[3]{0:T(128)S(1)}, s32[3]{0:T(128)}, u32[]{:S(2)}) copy-start(s32[3]{0:T(128)} %constant.460.clone.1) | copy-start | bytes 40
  1133.9 176.2 %copy-start.13 = (s32[3]{0:T(128)S(1)}, s32[3]{0:T(128)}, u32[]{:S(2)}) copy-start(s32[3]{0:T(128)} %constant.463.clone.1) | copy-start | bytes 40
  1133.9 177.0 %copy-start.12 = (s32[3]{0:T(128)S(1)}, s32[3]{0:T(128)}, u32[]{:S(2)}) copy-start(s32[3]{0:T(128)} %constant.465.clone.1) | copy-start | bytes 40
  1133.9 177.7 %copy-start.11 = (s32[3]{0:T(128)S(1)}, s32[3]{0:T(128)}, u32[]{:S(2)}) copy-start(s32[3]{0:T(128)} %constant.467.clone.1) | copy-start | bytes 40
  1133.9 178.5 %copy-start.10 = (s32[3]{0:T(128)S(1)}, s32[3]{0:T(128)}, u32[]{:S(2)}) copy-start(s32[3]{0:T(128)} %constant.469.clone.1) | copy-start | bytes 40
  1133.9 179.2 %copy-start.9 = (s32[3]{0:T(128)S(1)}, s32[3]{0:T(128)}, u32[]{:S(2)}) copy-start(s32[3]{0:T(128)} %constant.471.clone.1) | copy-start | bytes 40
  1133.9 237.6 %reduce-scatter.23.cloned.1.call-start = ((), (), s32[]{:S(2)}) async-start(), calls=%async_computation.15 | async-start | bytes 1179648 | tf_op jit(solution)/shard_map/reduce_scatter | solution.py:45
Sparse Core Ops, SparseCore 0:
  78.6 63.3 reduce-scatter.8
  249.7 62.9 reduce-scatter.10
  423.6 63.1 reduce-scatter.12
  600.8 63.0 reduce-scatter.14
  781.3 63.1 reduce-scatter.16
  959.1 63.1 reduce-scatter.18
  1134.0 63.1 reduce-scatter.20
  1308.3 63.1 reduce-scatter.22
where the time goes:
time: 1480 us; the launch traced here: 1470 us
  blocking collectives  740 us (50%)
  waiting for transfers between devices  476 us (32%)
  matrix products  168 us (11%)
  other arithmetic  38.8 us (3%)
  local copies, waits for them, and re-layouts  33.9 us (2%)
  between operations  14.8 us (1%)
    reduce_scatter x8, waiting for transfers between devices, apply_matrix(): lax.psum_scatter(jnp.einsum('mk,nki->mni', rows_onehot, products, precisi...  475 us
    psum x8, blocking collectives, body(): coeffs = lax.psum(local_dots, ('row', 'col'))  319 us
    psum x8, blocking collectives, body(): lax.psum(jnp.sum(candidate * candidate, axis=1), ('row', 'col'))  314 us
    dot_general x8, matrix products, apply_matrix(): jnp.einsum('kij,nkj->nki', blocks, picked, precision=lax.Precision.HIGHEST)  124 us
    all_gather x8, blocking collectives, apply_matrix(): gathered = lax.all_gather(vector, 'row', axis=1, tiled=True)  66.2 us
    psum x1, blocking collectives, body(): lax.psum(jnp.sum(right_sides * right_sides, axis=1), ('row', 'col'))  41.9 us
  transfers between devices with their start and end apart: 8, of which 8 were waited for; matrix products, arithmetic and copies ran while one was open for 2% of the time, Pallas kernels for 0%

commit v1 on v0

--- a/solution.py
+++ b/solution.py
@@ -73,7 +73,9 @@
         candidate = candidate - jnp.einsum(
             "ni,inl->nl", coeffs, stacked, precision=lax.Precision.HIGHEST
         )
-        remainder_sq = lax.psum(jnp.sum(candidate * candidate, axis=1), ("row", "col"))
+        part = jnp.sum(candidate * candidate, axis=1)
+        parts = lax.all_gather(part, ("row", "col"), axis=0, tiled=False)
+        remainder_sq = parts.sum(axis=0)
         new_norm = jnp.sqrt(remainder_sq + epsilon)
         hessenberg = hessenberg.at[:, : j + 1, j].set(coeffs)
         hessenberg = hessenberg.at[:, j + 1, j].set(new_norm)

time: 1480 us -> 1490 us (level)
    psum x8 -> x0, blocking collectives: 314 us -> none  [body(): lax.psum(jnp.sum(candidate * candidate, axis=1), ('row', 'col'))]
    unnamed x0 -> x8, blocking collectives: none -> 314 us
where the time goes in v1:
time: 1490 us; the launch traced here: 1480 us
  blocking collectives  741 us (50%)
  waiting for transfers between devices  473 us (32%)
  matrix products  168 us (11%)
  other arithmetic  42.3 us (3%)
  local copies, waits for them, and re-layouts  38.1 us (3%)
  between operations  15.2 us (1%)
    reduce_scatter x8, waiting for transfers between devices, apply_matrix(): lax.psum_scatter(jnp.einsum('mk,nki->mni', rows_onehot, products, precisi...  472 us
    psum x8, blocking collectives, body(): coeffs = lax.psum(local_dots, ('row', 'col'))  319 us
    unnamed x8, blocking collectives  314 us
    dot_general x8, matrix products, apply_matrix(): jnp.einsum('kij,nkj->nki', blocks, picked, precision=lax.Precision.HIGHEST)  124 us
    all_gather x8, blocking collectives, apply_matrix(): gathered = lax.all_gather(vector, 'row', axis=1, tiled=True)  66.5 us
    psum x1, blocking collectives, body(): lax.psum(jnp.sum(right_sides * right_sides, axis=1), ('row', 'col'))  41.9 us
  transfers between devices with their start and end apart: 8, of which 8 were waited for; matrix products, arithmetic and copies ran while one was open for 2% of the time, Pallas kernels for 0%

profile of v1, /device:TPU:0, one launch (start us, length us, event | category | flops | bytes accessed | tf_op | source)
XLA Modules:
  0.0 1477.4 jit_solution(2276228099475701489)
XLA Ops:
  9.7 41.9 %psum.63 = f32[2]{0:T(128)S(1)} all-reduce(f32[2]{0:T(128)S(1)} %multiply_reduce_fusion.8), channel_id=1, replica_groups=mesh['row'=4,'col'=8] {'row','col'}, use_global_device_ids=true, to_apply=%region_1.0 | all-reduce | flops 2 | bytes 16 | tf_op jit(solution)/shard_map/psum | solution.py:64
  82.4 59.4 %reduce-scatter.9.cloned.1.call-done = f32[128,2,128]{2,0,1:T(8,128)} async-done(((f32[1024,2,128]{2,0,1:T(8,128)}), f32[128,2,128]{2,0,1:T(8,128)}) %reduce-scatter.9.cloned.1.call-update) | async-done | bytes 131088 | tf_op jit(solution)/shard_map/reduce_scatter | solution.py:45
  142.9 39.9 %psum.64 = f32[2,1]{0,1:T(1,128)S(1)} all-reduce(f32[2,1]{0,1:T(1,128)S(1)} %bitcast.742), channel_id=1, replica_groups=mesh['row'=4,'col'=8] {'row','col'}, use_global_device_ids=true, to_apply=%region_3.5 | all-reduce | flops 2 | bytes 16 | tf_op jit(solution)/shard_map/psum | solution.py:72
  184.3 39.2 %all-reduce.1 = f32[64]{0:T(128)S(1)} all-reduce(f32[64]{0:T(128)S(1)} %dynamic-update-slice.48), channel_id=2, replica_groups=mesh['row'=4,'col'=8] {'row','col'}, use_global_device_ids=true, to_apply=%add.1 | all-reduce | flops 64 | bytes 512
  250.7 62.3 %reduce-scatter.11.cloned.1.call-done = f32[128,2,128]{2,0,1:T(8,128)} async-done(((f32[1024,2,128]{2,0,1:T(8,128)}), f32[128,2,128]{2,0,1:T(8,128)}) %reduce-scatter.11.cloned.1.call-update) | async-done | bytes 131088 | tf_op jit(solution)/shard_map/reduce_scatter | solution.py:45
  316.6 39.8 %psum.65 = f32[2,2]{1,0:T(2,128)S(1)} all-reduce(f32[2,2]{1,0:T(2,128)S(1)} %bitcast.732), channel_id=1, replica_groups=mesh['row'=4,'col'=8] {'row','col'}, use_global_device_ids=true, to_apply=%region_7.9 | all-reduce | flops 4 | bytes 32 | tf_op jit(solution)/shard_map/psum | solution.py:72
  357.9 39.3 %all-reduce.2 = f32[64]{0:T(128)S(1)} all-reduce(f32[64]{0:T(128)S(1)} %dynamic-update-slice.49), channel_id=3, replica_groups=mesh['row'=4,'col'=8] {'row','col'}, use_global_device_ids=true, to_apply=%add.2 | all-reduce | flops 64 | bytes 512
  425.4 62.3 %reduce-scatter.13.cloned.1.call-done = f32[128,2,128]{2,0,1:T(8,128)} async-done(((f32[1024,2,128]{2,0,1:T(8,128)}), f32[128,2,128]{2,0,1:T(8,128)}) %reduce-scatter.13.cloned.1.call-update) | async-done | bytes 131088 | tf_op jit(solution)/shard_map/reduce_scatter | solution.py:45
  491.2 39.8 %psum.66 = f32[2,3]{1,0:T(2,128)S(1)} all-reduce(f32[2,3]{1,0:T(2,128)S(1)} %bitcast.733), channel_id=1, replica_groups=mesh['row'=4,'col'=8] {'row','col'}, use_global_device_ids=true, to_apply=%region_12.14 | all-reduce | flops 6 | bytes 48 | tf_op jit(solution)/shard_map/psum | solution.py:72
  533.3 39.2 %all-reduce.3 = f32[64]{0:T(128)S(1)} all-reduce(f32[64]{0:T(128)S(1)} %dynamic-update-slice.50), channel_id=4, replica_groups=mesh['row'=4,'col'=8] {'row','col'}, use_global_device_ids=true, to_apply=%add.3 | all-reduce | flops 64 | bytes 512
  603.1 61.4 %reduce-scatter.15.cloned.1.call-done = f32[128,2,128]{2,0,1:T(8,128)} async-done(((f32[1024,2,128]{2,0,1:T(8,128)}), f32[128,2,128]{2,0,1:T(8,128)}) %reduce-scatter.15.cloned.1.call-update) | async-done | bytes 131088 | tf_op jit(solution)/shard_map/reduce_scatter | solution.py:45
  669.8 39.8 %psum.67 = f32[2,4]{1,0:T(2,128)S(1)} all-reduce(f32[2,4]{1,0:T(2,128)S(1)} %bitcast.734), channel_id=1, replica_groups=mesh['row'=4,'col'=8] {'row','col'}, use_global_device_ids=true, to_apply=%region_17.19 | all-reduce | flops 8 | bytes 64 | tf_op jit(solution)/shard_map/psum | solution.py:72
  714.0 39.2 %all-reduce.4 = f32[64]{0:T(128)} all-reduce(f32[64]{0:T(128)S(1)} %dynamic-update-slice.51), channel_id=5, replica_groups=mesh['row'=4,'col'=8] {'row','col'}, use_global_device_ids=true, to_apply=%add.4 | all-reduce | flops 64 | bytes 512
  786.8 61.9 %reduce-scatter.17.cloned.1.call-done = f32[128,2,128]{2,0,1:T(8,128)} async-done(((f32[1024,2,128]{2,0,1:T(8,128)}), f32[128,2,128]{2,0,1:T(8,128)}) %reduce-scatter.17.cloned.1.call-update) | async-done | bytes 131088 | tf_op jit(solution)/shard_map/reduce_scatter | solution.py:45
  853.2 39.8 %psum.68 = f32[2,5]{1,0:T(2,128)S(1)} all-reduce(f32[2,5]{1,0:T(2,128)S(1)} %bitcast.727), channel_id=1, replica_groups=mesh['row'=4,'col'=8] {'row','col'}, use_global_device_ids=true, to_apply=%region_22.24 | all-reduce | flops 10 | bytes 80 | tf_op jit(solution)/shard_map/psum | solution.py:72
  896.4 39.2 %all-reduce.5 = f32[64]{0:T(128)S(1)} all-reduce(f32[64]{0:T(128)S(1)} %dynamic-update-slice.52), channel_id=6, replica_groups=mesh['row'=4,'col'=8] {'row','col'}, use_global_device_ids=true, to_apply=%add.5 | all-reduce | flops 64 | bytes 512
  964.4 63.1 %reduce-scatter.19.cloned.1.call-done = f32[128,2,128]{2,0,1:T(8,128)} async-done(((f32[1024,2,128]{2,0,1:T(8,128)}), f32[128,2,128]{2,0,1:T(8,128)}) %reduce-scatter.19.cloned.1.call-update) | async-done | bytes 131088 | tf_op jit(solution)/shard_map/reduce_scatter | solution.py:45
  1031.5 39.8 %psum.69 = f32[2,6]{1,0:T(2,128)S(1)} all-reduce(f32[2,6]{1,0:T(2,128)S(1)} %bitcast.728), channel_id=1, replica_groups=mesh['row'=4,'col'=8] {'row','col'}, use_global_device_ids=true, to_apply=%region_27.29 | all-reduce | flops 12 | bytes 96 | tf_op jit(solution)/shard_map/psum | solution.py:72
  1073.2 39.2 %all-reduce.6 = f32[64]{0:T(128)S(1)} all-reduce(f32[64]{0:T(128)S(1)} %dynamic-update-slice.53), channel_id=7, replica_groups=mesh['row'=4,'col'=8] {'row','col'}, use_global_device_ids=true, to_apply=%add.6 | all-reduce | flops 64 | bytes 512
  1138.8 63.2 %reduce-scatter.21.cloned.1.call-done = f32[128,2,128]{2,0,1:T(8,128)} async-done(((f32[1024,2,128]{2,0,1:T(8,128)}), f32[128,2,128]{2,0,1:T(8,128)}) %reduce-scatter.21.cloned.1.call-update) | async-done | bytes 131088 | tf_op jit(solution)/shard_map/reduce_scatter | solution.py:45
  1206.0 39.8 %psum.70 = f32[2,7]{1,0:T(2,128)S(1)} all-reduce(f32[2,7]{1,0:T(2,128)S(1)} %bitcast.729), channel_id=1, replica_groups=mesh['row'=4,'col'=8] {'row','col'}, use_global_device_ids=true, to_apply=%region_32.34 | all-reduce | flops 14 | bytes 112 | tf_op jit(solution)/shard_map/psum | solution.py:72
  1247.7 39.2 %all-reduce.7 = f32[64]{0:T(128)S(1)} all-reduce(f32[64]{0:T(128)S(1)} %dynamic-update-slice.54), channel_id=8, replica_groups=mesh['row'=4,'col'=8] {'row','col'}, use_global_device_ids=true, to_apply=%add.7 | all-reduce | flops 64 | bytes 512
  1380.5 40.1 %psum.71 = f32[2,8]{1,0:T(2,128)S(1)} all-reduce(f32[2,8]{1,0:T(2,128)S(1)} %bitcast.726), channel_id=1, replica_groups=mesh['row'=4,'col'=8] {'row','col'}, use_global_device_ids=true, to_apply=%region_37.39 | all-reduce | flops 16 | bytes 128 | tf_op jit(solution)/shard_map/psum | solution.py:72
  1423.6 39.2 %all-reduce.8 = f32[64]{0:T(128)S(1)} all-reduce(f32[64]{0:T(128)S(1)} %dynamic-update-slice.55), channel_id=9, replica_groups=mesh['row'=4,'col'=8] {'row','col'}, use_global_device_ids=true, to_apply=%add.8 | all-reduce | flops 64 | bytes 512
  (243 shorter events, 354.2 us)
Async XLA Ops:
  7.2 69.7 %copy-start.9 = (s32[1,128]{1,0:T(1,128)S(1)}, s32[1,128]{1,0:T(1,128)}, u32[]{:S(2)}) copy-start(s32[1,128]{1,0:T(1,128)} %param.40) | copy-start | bytes 1540
  7.2 134.6 %copy-start = (f32[16384]{0:T(1024)S(1)}, f32[16384]{0:T(1024)}, u32[]{:S(2)}) copy-start(f32[16384]{0:T(1024)} %param.42) | copy-start | bytes 196612
  7.2 134.6 %reduce-scatter.9.cloned.1.call-start = ((), (), s32[]{:S(2)}) async-start(), calls=%async_computation.8 | async-start | bytes 1179648 | tf_op jit(solution)/shard_map/reduce_scatter | solution.py:45
  78.5 234.6 %reduce-scatter.11.cloned.1.call-start = ((), (), s32[]{:S(2)}) async-start(), calls=%async_computation.9 | async-start | bytes 1179648 | tf_op jit(solution)/shard_map/reduce_scatter | solution.py:45
  249.8 238.0 %reduce-scatter.13.cloned.1.call-start = ((), (), s32[]{:S(2)}) async-start(), calls=%async_computation.10 | async-start | bytes 1179648 | tf_op jit(solution)/shard_map/reduce_scatter | solution.py:45
  424.4 240.1 %reduce-scatter.15.cloned.1.call-start = ((), (), s32[]{:S(2)}) async-start(), calls=%async_computation.11 | async-start | bytes 1179648 | tf_op jit(solution)/shard_map/reduce_scatter | solution.py:45
  532.2 0.7 copy-start.6
  573.8 28.3 %copy-start.2 = (f32[2,16384]{1,0:T(2,128)}, f32[2,16384]{1,0:T(2,128)S(1)}, u32[]{:S(2)}) copy-start(f32[2,16384]{1,0:T(2,128)S(1)} %get-tuple-element.259) | copy-start | bytes 393220
  601.2 247.5 %reduce-scatter.17.cloned.1.call-start = ((), (), s32[]{:S(2)}) async-start(), calls=%async_computation.12 | async-start | bytes 1179648 | tf_op jit(solution)/shard_map/reduce_scatter | solution.py:45
  603.1 182.7 %copy-start.1 = (f32[7,2,16384]{2,1,0:T(2,128)S(1)}, f32[7,2,16384]{2,1,0:T(2,128)}, u32[]{:S(2)}) copy-start(f32[7,2,16384]{2,1,0:T(2,128)} %get-tuple-element.273) | copy-start | bytes 2752516
  665.6 0.7 copy-start.5
  756.7 0.7 copy-start.3
  785.7 241.8 %reduce-scatter.19.cloned.1.call-start = ((), (), s32[]{:S(2)}) async-start(), calls=%async_computation.13 | async-start | bytes 1179648 | tf_op jit(solution)/shard_map/reduce_scatter | solution.py:45
  849.9 0.7 copy-start.4
  964.3 237.7 %reduce-scatter.21.cloned.1.call-start = ((), (), s32[]{:S(2)}) async-start(), calls=%async_computation.14 | async-start | bytes 1179648 | tf_op jit(solution)/shard_map/reduce_scatter | solution.py:45
  1138.6 175.9 %copy-start.17 = (s32[3]{0:T(128)S(1)}, s32[3]{0:T(128)}, u32[]{:S(2)}) copy-start(s32[3]{0:T(128)} %constant.460.clone.1) | copy-start | bytes 40
  1138.6 176.6 %copy-start.16 = (s32[3]{0:T(128)S(1)}, s32[3]{0:T(128)}, u32[]{:S(2)}) copy-start(s32[3]{0:T(128)} %constant.463.clone.1) | copy-start | bytes 40
  1138.6 177.3 %copy-start.15 = (s32[3]{0:T(128)S(1)}, s32[3]{0:T(128)}, u32[]{:S(2)}) copy-start(s32[3]{0:T(128)} %constant.465.clone.1) | copy-start | bytes 40
  1138.6 178.1 %copy-start.14 = (s32[3]{0:T(128)S(1)}, s32[3]{0:T(128)}, u32[]{:S(2)}) copy-start(s32[3]{0:T(128)} %constant.467.clone.1) | copy-start | bytes 40
  1138.6 178.9 %copy-start.13 = (s32[3]{0:T(128)S(1)}, s32[3]{0:T(128)}, u32[]{:S(2)}) copy-start(s32[3]{0:T(128)} %constant.469.clone.1) | copy-start | bytes 40
  1138.7 179.6 %copy-start.12 = (s32[3]{0:T(128)S(1)}, s32[3]{0:T(128)}, u32[]{:S(2)}) copy-start(s32[3]{0:T(128)} %constant.471.clone.1) | copy-start | bytes 40
  1138.7 188.9 %copy-start.10 = (f32[2,1,1]{0,2,1:T(1,128)S(1)}, f32[2,1,1]{0,2,1:T(1,128)}, u32[]{:S(2)}) copy-start(f32[2,1,1]{0,2,1:T(1,128)} %get-tuple-element.300) | copy-start | bytes 28
  1138.7 192.2 %copy-start.11 = (f32[2,1,1]{0,2,1:T(1,128)S(1)}, f32[2,1,1]{0,2,1:T(1,128)}, u32[]{:S(2)}) copy-start(f32[2,1,1]{0,2,1:T(1,128)} %get-tuple-element.296) | copy-start | bytes 28
  1138.7 237.7 %reduce-scatter.23.cloned.1.call-start = ((), (), s32[]{:S(2)}) async-start(), calls=%async_computation.15 | async-start | bytes 1179648 | tf_op jit(solution)/shard_map/reduce_scatter | solution.py:45
  (2 other events, 1.3 us)
Sparse Core Ops, SparseCore 0:
  78.6 63.1 reduce-scatter.8
  249.9 63.1 reduce-scatter.10
  424.5 63.1 reduce-scatter.12
  601.3 63.1 reduce-scatter.14
  785.9 62.8 reduce-scatter.16
  964.4 63.0 reduce-scatter.18
  1138.8 63.0 reduce-scatter.20
  1313.4 63.0 reduce-scatter.22
